TPU v7x, 32 devices: a whole 2x2x4 slice. The times are simulated.
32 devices in a mesh: section: 2 (over core), dp: 8 (over z, x), tensor: 2 (over y).
Axes of the slice: x: 2, y: 2, z: 4, core: 2. Of those that a mesh axis runs over, the one named last changes fastest.
Arguments:
- tokens: bfloat16 [1024, 4096], P('dp', 'tensor'), may hold values from -6 to 6
- gain: bfloat16 [2, 4096], P('section', 'tensor'), may hold values from 0.099609375 to 1.8984375
- w_up: bfloat16 [2, 4096, 5120], P('section', 'dp', 'tensor'), may hold values from -0.09375 to 0.09375
- w_down: bfloat16 [2, 5120, 4096], P('section', 'tensor', 'dp'), may hold values from -0.078125 to 0.078125
- cotangent: bfloat16 [2, 1024, 4096], P('section', 'dp'), may hold values from -6 to 6
Outputs:
- states: bfloat16 [2, 1024, 4096], P('section', 'dp', 'tensor')
- grad_down: bfloat16 [2, 5120, 4096], P('section', 'tensor', 'dp')
All inputs are finite; a program needn't handle non-finite values.
Results may differ from a plain program's by a relative error of at most 0.02.
Values may be sent and summed in bfloat16 or wider, within the bound.
A program may use at most 128 MiB of HBM per device.

v0:
```python
import jax
import jax.numpy as jnp
from jax import lax
from jax.sharding import PartitionSpec as P

EPS = 1e-06
F32 = jnp.float32
BF16 = jnp.bfloat16


def body(tokens, gain, w_up, w_down, cotangent):
    core = lax.axis_index("section")
    layers = lax.axis_size("section")
    assert layers == 2
    dp_id = lax.axis_index("dp")
    dp_count = lax.axis_size("dp")
    tensor_id = lax.axis_index("tensor")
    tensor_count = lax.axis_size("tensor")
    rows, own_width = tokens.shape
    width = own_width * tensor_count
    slice_width = width // dp_count
    hidden_width = w_up.shape[2]
    half = hidden_width // layers
    other = 1 - core
    all_rows = rows * dp_count

    def swap(array):
        return lax.ppermute(array, "section", [(0, 1), (1, 0)])

    def both(own, got):
        return (jnp.where(core == 0, own, got), jnp.where(core == 0, got, own))

    cot_mine = lax.all_to_all(cotangent[0], "dp", split_axis=1, concat_axis=0, tiled=True)
    half_rows = rows // layers
    tok_half = lax.dynamic_slice_in_dim(tokens, core * half_rows, half_rows, 0)
    tok_full = lax.all_gather(tok_half, "tensor", axis=1, tiled=True)
    tok_f = tok_full.astype(F32)
    sums_half = jnp.sum(tok_f * tok_f, axis=1)
    sums_a, sums_b = both(sums_half, swap(sums_half))
    sums = jnp.concatenate([sums_a, sums_b])
    x_half = lax.all_to_all(tok_full, "dp", split_axis=1, concat_axis=0, tiled=True)
    x_a, x_b = both(x_half, swap(x_half))
    x = jnp.concatenate(
        [
            x_a.reshape(dp_count, half_rows, slice_width),
            x_b.reshape(dp_count, half_rows, slice_width),
        ],
        axis=1,
    ).reshape(all_rows, slice_width)
    gain_all = lax.all_gather(gain, "tensor", axis=1, tiled=True)
    gain_own = lax.dynamic_slice_in_dim(gain_all, dp_id * slice_width, slice_width, 1)
    gains = both(gain_own, swap(gain_own))
    up_parts = both(
        lax.dynamic_slice_in_dim(w_up[0], core * half, half, 1),
        swap(lax.dynamic_slice_in_dim(w_up[0], other * half, half, 1)),
    )
    down_parts = both(
        lax.dynamic_slice_in_dim(w_down[0], core * half, half, 0),
        swap(lax.dynamic_slice_in_dim(w_down[0], other * half, half, 0)),
    )
    states = []
    hiddens = []
    for layer in range(layers):
        x_f = x.astype(F32)
        if layer > 0:
            sums = lax.psum_scatter(
                jnp.sum(x_f * x_f, axis=1), "dp", scatter_dimension=0, tiled=True
            )
        scaled = (x_f * gains[layer].astype(F32)).astype(BF16)
        part = jnp.dot(scaled, up_parts[layer], preferred_element_type=F32).astype(BF16)
        pre = lax.psum_scatter(part, "dp", scatter_dimension=0, tiled=True)
        inverse_rms = lax.rsqrt(sums / width + EPS)
        hidden = jax.nn.gelu(pre.astype(F32) * inverse_rms[:, None], approximate=True).astype(BF16)
        hidden_all = lax.all_gather(hidden, "dp", axis=0, tiled=True)
        hiddens.append(hidden_all)
        out = jnp.dot(hidden_all, down_parts[layer], preferred_element_type=F32)
        mid = all_rows // layers
        keep = lax.dynamic_slice_in_dim(out, core * mid, mid, 0)
        give = lax.dynamic_slice_in_dim(out, other * mid, mid, 0).astype(BF16)
        summed = keep + swap(give).astype(F32)
        if tensor_count == 2:
            sent = summed.astype(BF16)
            got = lax.ppermute(sent, "tensor", [(0, 1), (1, 0)])
            summed = sent.astype(F32) + got.astype(F32)
        else:
            summed = lax.psum(summed.astype(BF16), "tensor").astype(F32)
        x_mid = lax.dynamic_slice_in_dim(x_f, core * mid, mid, 0)
        new_mid = (x_mid + summed).astype(BF16)
        new_a, new_b = both(new_mid, swap(new_mid))
        x = jnp.concatenate([new_a, new_b], axis=0)
        states.append(x)
    state_own = jnp.where(core == 0, states[0], states[1])
    state_rows = lax.all_to_all(state_own, "dp", split_axis=0, concat_axis=1, tiled=True)
    state = lax.dynamic_slice_in_dim(state_rows, tensor_id * own_width, own_width, 1)
    hid_keep = jnp.where(core == 0, hiddens[0], hiddens[1])
    hid_got = swap(jnp.where(core == 0, hiddens[1], hiddens[0]))
    hid_parts = both(hid_keep, hid_got)
    hidden_whole = jnp.concatenate(hid_parts, axis=1)
    grad = lax.dot_general(
        hidden_whole, cot_mine, (((0,), (0,)), ((), ())), preferred_element_type=F32
    ).astype(BF16)
    return (state[None], grad[None])


def solution(mesh):
    placed = (
        P("dp", "tensor"),
        P("section", "tensor"),
        P("section", "dp", "tensor"),
        P("section", "tensor", "dp"),
        P("section", "dp", None),
    )
    return jax.shard_map(
        body,
        mesh=mesh,
        in_specs=placed,
        out_specs=(P("section", "dp", "tensor"), P("section", "tensor", "dp")),
        check_vma=False,
    )
```

profile of v0, /device:TPU:0, one launch (start us, length us, event | category | flops | bytes accessed | tf_op | source)
XLA Modules:
  0.0 413.5 jit_solution(5616129061812105178)
XLA Ops:
  8.2 10.0 %all_gather.12 = bf16[64,4096]{1,0:T(8,128)(2,1)S(1)} all-gather(bf16[64,2048]{1,0:T(8,128)(2,1)S(1)} %constant_dynamic-slice_fusion.2), channel_id=1, replica_groups=mesh['section'=2,'dp'=8,'tensor'=2] {'tensor'}, dimensions={1}, use_global_device_ids=true | all-gather | bytes 786432 | tf_op jit(solution)/shard_map/all_gather | solution.py:36
  19.0 6.2 %all-to-all-start = ((bf16[64,8,512]{2,0,1:T(8,128)(2,1)}), bf16[64,8,512]{2,0,1:T(8,128)(2,1)S(1)}, u32[]{:S(2)}, u32[]{:S(2)}) async-start(bf16[64,8,512]{2,0,1:T(8,128)(2,1)} %bitcast.43), calls=%async_computation | async-start | bytes 1048576 | tf_op jit(solution)/shard_map/all_to_all | solution.py:41
  25.3 2.5 dynamic-slice_bitcast_fusion.1
  27.7 11.2 %all-to-all-done = bf16[64,8,512]{2,0,1:T(8,128)(2,1)S(1)} async-done(((bf16[64,8,512]{2,0,1:T(8,128)(2,1)}), bf16[64,8,512]{2,0,1:T(8,128)(2,1)S(1)}, u32[]{:S(2)}, u32[]{:S(2)}) %all-to-all-start) | async-done | bytes 524320 | tf_op jit(solution)/shard_map/all_to_all | solution.py:41
  38.9 4.3 %all_gather.13 = bf16[1,4096]{1,0:T(2,128)(2,1)S(1)} all-gather(bf16[1,2048]{1,0:T(2,128)(2,1)S(1)} %copy-done.12), channel_id=1, replica_groups=mesh['section'=2,'dp'=8,'tensor'=2] {'tensor'}, dimensions={1}, use_global_device_ids=true | all-gather | bytes 12288 | tf_op jit(solution)/shard_map/all_gather | solution.py:50
  46.4 3.1 convolution_convert_fusion.1
  52.2 68.8 %reduce-scatter.3.cloned.1.call-done = bf16[128,1280]{1,0:T(8,128)(2,1)} async-done(((bf16[1024,1280]{1,0:T(8,128)(2,1)}), bf16[128,1280]{1,0:T(8,128)(2,1)}) %reduce-scatter.3.cloned.1.call-update) | async-done | bytes 327696 | tf_op jit(solution)/shard_map/reduce_scatter | solution.py:71
  120.9 2.0 fusion.30
  123.0 2.5 dynamic-slice_bitcast_fusion
  125.5 3.4 collective-permute-done.4
  128.9 48.4 %all-gather.3.cloned.1.call-done = bf16[1024,1280]{1,0:T(8,128)(2,1)} async-done(((bf16[128,1280]{1,0:T(8,128)(2,1)}), bf16[1024,1280]{1,0:T(8,128)(2,1)}) %all-gather.3.cloned.1.call-update) | async-done | bytes 2621456 | tf_op jit(solution)/shard_map/all_gather | solution.py:74
  177.3 3.7 fusion.10
  183.1 2.1 collective-permute-done.5
  188.2 12.5 %collective-permute-done.6 = bf16[512,512]{1,0:T(8,128)(2,1)S(1)} collective-permute-done((bf16[512,512]{1,0:T(8,128)(2,1)S(1)}, bf16[512,512]{1,0:T(8,128)(2,1)S(1)}, u32[]{:S(2)}, u32[]{:S(2)}) %collective-permute-start.6) | collective-permute-done | bytes 524320 | tf_op jit(solution)/shard_map/ppermute | solution.py:83
  201.0 1.9 collective-permute-done.7
  203.0 4.8 %convolution_convert_fusion = bf16[1024,1280]{1,0:T(8,128)(2,1)} fusion(bf16[512,1280]{1,0:T(8,128)(2,1)} %collective-permute-done.2, pred[]{:T(512)S(6)} %eq.2, bf16[1,512,2560]{2,1,0:T(8,128)(2,1)S(1)} %copy-done.11, s32[]{:T(128)S(6)} %select_n.145, f32[512]{0:T(512)S(1)} %bitcast.52, bf16[512,512]{1,0:T(8,128)(2,1)S(1)} %get-tuple-element.7, ...), kind=kOutput, calls=%fused_computation.6 | convolution fusion | flops 1347289088 | bytes 6293509 | tf_op jit(solution)/shard_map/dot_general | solution.py:70
  209.9 19.5 %all-reduce = f32[1024]{0:T(1024)S(1)} all-reduce(f32[1024]{0:T(1024)S(1)} %multiply_reduce_fusion), channel_id=4, replica_groups=mesh['section'=2,'dp'=8,'tensor'=2] {'dp'}, use_global_device_ids=true, to_apply=%region_4.5.clone | all-reduce | flops 1024 | bytes 8192
  229.5 48.0 %reduce-scatter.5.cloned.1.call-done = bf16[128,1280]{1,0:T(8,128)(2,1)} async-done(((bf16[1024,1280]{1,0:T(8,128)(2,1)}), bf16[128,1280]{1,0:T(8,128)(2,1)}) %reduce-scatter.5.cloned.1.call-update) | async-done | bytes 327696 | tf_op jit(solution)/shard_map/reduce_scatter | solution.py:71
  277.5 2.0 fusion.38
  279.5 54.1 %all-gather.5.cloned.1.call-done = bf16[1024,1280]{1,0:T(8,128)(2,1)} async-done(((bf16[128,1280]{1,0:T(8,128)(2,1)}), bf16[1024,1280]{1,0:T(8,128)(2,1)}) %all-gather.5.cloned.1.call-update) | async-done | bytes 2621456 | tf_op jit(solution)/shard_map/all_gather | solution.py:74
  333.7 4.2 %fusion.11 = f32[1024,512]{1,0:T(8,128)S(1)} fusion(bf16[1024,1280]{1,0:T(8,128)(2,1)} %all-gather.5.cloned.1.call-done, bf16[1280,512]{1,0:T(8,128)(2,1)} %collective-permute-done.4, pred[]{:T(512)S(6)} %eq.2, bf16[1,2560,512]{2,1,0:T(8,128)(2,1)} %param.8, s32[]{:T(128)S(6)} %select_n.145), kind=kOutput, calls=%fused_computation.18 | convolution fusion | flops 1342832640 | bytes 7340037 | tf_op jit(solution)/shard_map/dot_general | solution.py:76
  342.4 2.3 copy.18
  344.7 4.2 %all-to-all-start.2 = ((bf16[128,8,512]{0,2,1:T(8,128)(2,1)}), bf16[128,8,512]{0,2,1:T(8,128)(2,1)}, u32[]{:S(2)}, u32[]{:S(2)}) async-start(bf16[128,8,512]{0,2,1:T(8,128)(2,1)} %bitcast.45), calls=%async_computation.4 | async-start | bytes 2097152 | tf_op jit(solution)/shard_map/all_to_all | solution.py:33
  352.4 12.1 %collective-permute-done.9 = bf16[512,512]{1,0:T(8,128)(2,1)S(1)} collective-permute-done((bf16[512,512]{1,0:T(8,128)(2,1)S(1)}, bf16[512,512]{1,0:T(8,128)(2,1)S(1)}, u32[]{:S(2)}, u32[]{:S(2)}) %collective-permute-start.9) | collective-permute-done | bytes 524320 | tf_op jit(solution)/shard_map/ppermute | solution.py:83
  364.8 1.9 collective-permute-done.10
  368.0 2.3 copy.16
  370.3 4.8 %all-to-all-done.2 = bf16[128,8,512]{0,2,1:T(8,128)(2,1)} async-done(((bf16[128,8,512]{0,2,1:T(8,128)(2,1)}), bf16[128,8,512]{0,2,1:T(8,128)(2,1)}, u32[]{:S(2)}, u32[]{:S(2)}) %all-to-all-start.2) | async-done | bytes 1048608 | tf_op jit(solution)/shard_map/all_to_all | solution.py:33
  375.1 4.4 %all-to-all-start.1 = ((bf16[8,128,512]{1,2,0:T(8,128)(2,1)}), bf16[8,128,512]{1,2,0:T(8,128)(2,1)}, u32[]{:S(2)}, u32[]{:S(2)}) async-start(bf16[8,128,512]{1,2,0:T(8,128)(2,1)} %copy.16), calls=%async_computation.3 | async-start | bytes 2097152 | tf_op jit(solution)/shard_map/all_to_all | solution.py:93
  379.6 2.3 copy.19
  381.8 2.3 broadcast_select_fusion.1
  384.1 4.3 %fusion.7 = bf16[1,2560,512]{2,1,0:T(8,128)(2,1)} fusion(bf16[1024,512]{1,0:T(8,128)(2,1)S(1)} %bitcast.50, bf16[1024,1280]{1,0:T(8,128)(2,1)S(1)} %get-tuple-element.3, bf16[1024,1280]{1,0:T(8,128)(2,1)S(1)} %get-tuple-element.2), kind=kOutput, calls=%fused_computation.5 | convolution fusion | flops 2696151040 | bytes 8912896 | tf_op jit(solution)/shard_map/dot_general | solution.py:99
  388.4 16.5 %all-to-all-done.1 = bf16[8,128,512]{1,2,0:T(8,128)(2,1)} async-done(((bf16[8,128,512]{1,2,0:T(8,128)(2,1)}), bf16[8,128,512]{1,2,0:T(8,128)(2,1)}, u32[]{:S(2)}, u32[]{:S(2)}) %all-to-all-start.1) | async-done | bytes 1048608 | tf_op jit(solution)/shard_map/all_to_all | solution.py:93
  (80 shorter events, 26.6 us)
Async XLA Ops:
  7.2 1.0 copy-start
  19.0 19.8 %copy-start.12 = (bf16[1,2048]{1,0:T(2,128)(2,1)S(1)}, bf16[1,2048]{1,0:T(2,128)(2,1)}, u32[]{:S(2)}) copy-start(bf16[1,2048]{1,0:T(2,128)(2,1)} %param.6) | copy-start | bytes 12292
  19.0 19.8 %all-to-all-start = ((bf16[64,8,512]{2,0,1:T(8,128)(2,1)}), bf16[64,8,512]{2,0,1:T(8,128)(2,1)S(1)}, u32[]{:S(2)}, u32[]{:S(2)}) async-start(bf16[64,8,512]{2,0,1:T(8,128)(2,1)} %bitcast.43), calls=%async_computation | async-start | bytes 1048576 | tf_op jit(solution)/shard_map/all_to_all | solution.py:41
  25.2 95.7 %reduce-scatter.3.cloned.1.call-start = ((), (), s32[]{:S(2)}) async-start(), calls=%async_computation.5 | async-start | bytes 2949120 | tf_op jit(solution)/shard_map/reduce_scatter | solution.py:71
  27.7 17.3 %collective-permute-start.2 = (bf16[512,1280]{1,0:T(8,128)(2,1)}, bf16[512,1280]{1,0:T(8,128)(2,1)}, u32[]{:S(2)}, u32[]{:S(2)}) collective-permute-start(bf16[512,1280]{1,0:T(8,128)(2,1)} %dynamic-slice_bitcast_fusion.1), channel_id=1, source_target_pairs={{0,16},{16,0},{1,17},{17,1},{2,18},{18,2},{3,19},{19,3},{4,20},{20... | collective-permute-start | bytes 3932168 | tf_op jit(solution)/shard_map/ppermute | solution.py:28
  38.9 5.6 %collective-permute-start = (bf16[512,512]{1,0:T(8,128)(2,1)S(1)}, bf16[512,512]{1,0:T(8,128)(2,1)S(1)}, u32[]{:S(2)}, u32[]{:S(2)}) collective-permute-start(bf16[512,512]{1,0:T(8,128)(2,1)S(1)} %bitcast.47), channel_id=1, source_target_pairs={{0,16},{16,0},{1,17},{17,1},{2,18},{18,2},{3,19},{19,3},{4,20},{20... | collective-permute-start | bytes 1572872 | tf_op jit(solution)/shard_map/ppermute | solution.py:28
  43.2 1.2 collective-permute-start.1
  44.6 1.7 copy-start.10
  49.5 127.8 %all-gather.3.cloned.1.call-start = ((), (), s32[]{:S(2)}) async-start(), calls=%async_computation.6 | async-start | bytes 2949120 | tf_op jit(solution)/shard_map/all_gather | solution.py:74
  49.7 2.3 collective-permute-start.3
  123.0 154.5 %reduce-scatter.5.cloned.1.call-start = ((), (), s32[]{:S(2)}) async-start(), calls=%async_computation.7 | async-start | bytes 2949120 | tf_op jit(solution)/shard_map/reduce_scatter | solution.py:71
  125.5 3.4 collective-permute-start.4
  180.9 1.3 copy-start.8
  183.1 2.1 collective-permute-start.5
  186.6 16.3 %copy-start.11 = (bf16[1,512,2560]{2,1,0:T(8,128)(2,1)S(1)}, bf16[1,512,2560]{2,1,0:T(8,128)(2,1)}, u32[]{:S(2)}) copy-start(bf16[1,512,2560]{2,1,0:T(8,128)(2,1)} %param.7) | copy-start | bytes 7864324
  186.7 14.0 %collective-permute-start.6 = (bf16[512,512]{1,0:T(8,128)(2,1)S(1)}, bf16[512,512]{1,0:T(8,128)(2,1)S(1)}, u32[]{:S(2)}, u32[]{:S(2)}) collective-permute-start(bf16[512,512]{1,0:T(8,128)(2,1)S(1)} %add_convert_fusion.3), channel_id=1, source_target_pairs={{0,1},{1,0},{2,3},{3,2},{4,5},{5,4},{6,7},{7,6},{8,9},{9,8},{10,11... | collective-permute-start | bytes 1572872 | tf_op jit(solution)/shard_map/ppermute | solution.py:83
  200.9 2.0 collective-permute-start.7
  203.0 6.7 %copy-start.3 = (bf16[512,512]{1,0:T(8,128)(2,1)}, bf16[512,512]{1,0:T(8,128)(2,1)S(1)}, u32[]{:S(2)}) copy-start(bf16[512,512]{1,0:T(8,128)(2,1)S(1)} %get-tuple-element.6) | copy-start | bytes 1572868
  203.0 6.7 %copy-start.5 = (bf16[512,512]{1,0:T(8,128)(2,1)}, bf16[512,512]{1,0:T(8,128)(2,1)S(1)}, u32[]{:S(2)}) copy-start(bf16[512,512]{1,0:T(8,128)(2,1)S(1)} %get-tuple-element.7) | copy-start | bytes 1572868
  207.8 125.9 %all-gather.5.cloned.1.call-start = ((), (), s32[]{:S(2)}) async-start(), calls=%async_computation.8 | async-start | bytes 2949120 | tf_op jit(solution)/shard_map/all_gather | solution.py:74
  333.6 6.4 %copy-start.1 = (bf16[1024,1280]{1,0:T(8,128)(2,1)S(1)}, bf16[1024,1280]{1,0:T(8,128)(2,1)}, u32[]{:S(2)}) copy-start(bf16[1024,1280]{1,0:T(8,128)(2,1)} %all-gather.3.cloned.1.call-done) | copy-start | bytes 7864324
  333.6 6.4 %copy-start.2 = (bf16[1024,1280]{1,0:T(8,128)(2,1)S(1)}, bf16[1024,1280]{1,0:T(8,128)(2,1)}, u32[]{:S(2)}) copy-start(bf16[1024,1280]{1,0:T(8,128)(2,1)} %all-gather.5.cloned.1.call-done) | copy-start | bytes 7864324
  337.8 1.3 copy-start.7
  340.0 8.9 %collective-permute-start.8 = (bf16[512,512]{1,0:T(8,128)(2,1)}, bf16[512,512]{1,0:T(8,128)(2,1)}, u32[]{:S(2)}, u32[]{:S(2)}) collective-permute-start(bf16[512,512]{1,0:T(8,128)(2,1)} %dynamic-slice_convert_fusion), channel_id=1, source_target_pairs={{0,16},{16,0},{1,17},{17,1},{2,18},{18,2},{3,19},{19,3},{4,20},{20... | collective-permute-start | bytes 1572872 | tf_op jit(solution)/shard_map/ppermute | solution.py:28
  341.9 40.0 %collective-permute-start.11 = (bf16[1024,1280]{1,0:T(8,128)(2,1)}, bf16[1024,1280]{1,0:T(8,128)(2,1)}, u32[]{:S(2)}, u32[]{:S(2)}) collective-permute-start(bf16[1024,1280]{1,0:T(8,128)(2,1)} %broadcast_select_fusion.2), channel_id=1, source_target_pairs={{0,16},{16,0},{1,17},{17,1},{2,18},{18,2},{3,19},{19,3},{4,20},{20... | collective-permute-start | bytes 7864328 | tf_op jit(solution)/shard_map/ppermute | solution.py:28
  344.7 30.5 %all-to-all-start.2 = ((bf16[128,8,512]{0,2,1:T(8,128)(2,1)}), bf16[128,8,512]{0,2,1:T(8,128)(2,1)}, u32[]{:S(2)}, u32[]{:S(2)}) async-start(bf16[128,8,512]{0,2,1:T(8,128)(2,1)} %bitcast.45), calls=%async_computation.4 | async-start | bytes 2097152 | tf_op jit(solution)/shard_map/all_to_all | solution.py:33
  348.9 3.2 copy-start.4
  348.9 3.2 copy-start.6
  350.6 13.9 %collective-permute-start.9 = (bf16[512,512]{1,0:T(8,128)(2,1)S(1)}, bf16[512,512]{1,0:T(8,128)(2,1)S(1)}, u32[]{:S(2)}, u32[]{:S(2)}) collective-permute-start(bf16[512,512]{1,0:T(8,128)(2,1)S(1)} %add_convert_fusion.1), channel_id=1, source_target_pairs={{0,1},{1,0},{2,3},{3,2},{4,5},{5,4},{6,7},{7,6},{8,9},{9,8},{10,11... | collective-permute-start | bytes 1572872 | tf_op jit(solution)/shard_map/ppermute | solution.py:83
  364.7 2.0 collective-permute-start.10
  375.1 29.8 %all-to-all-start.1 = ((bf16[8,128,512]{1,2,0:T(8,128)(2,1)}), bf16[8,128,512]{1,2,0:T(8,128)(2,1)}, u32[]{:S(2)}, u32[]{:S(2)}) async-start(bf16[8,128,512]{1,2,0:T(8,128)(2,1)} %copy.16), calls=%async_computation.3 | async-start | bytes 2097152 | tf_op jit(solution)/shard_map/all_to_all | solution.py:93
  381.8 2.3 copy-start.9
  (1 other events, 0.7 us)
Sparse Core Ops, SparseCore 0:
  49.6 71.2 reduce-scatter.2
  123.7 53.5 all-gather.2
  207.9 69.5 reduce-scatter.4
  280.1 53.4 all-gather.4
where the time goes:
time: 414 us; the launch traced here: 413 us
  waiting for transfers between devices  288 us (70%)
  blocking collectives  33.8 us (8%)
  local copies, waits for them, and re-layouts  22.6 us (5%)
  starting transfers between devices  20.3 us (5%)
  matrix products  20 us (5%)
  between operations  14.7 us (4%)
  other arithmetic  14.5 us (4%)
    reduce_scatter x2, waiting for transfers between devices, body(): pre = lax.psum_scatter(part, 'dp', scatter_dimension=0, tiled=True)  117 us
    all_gather x2, waiting for transfers between devices, body(): hidden_all = lax.all_gather(hidden, 'dp', axis=0, tiled=True)  103 us
    ppermute x2, waiting for transfers between devices, body(): got = lax.ppermute(sent, 'tensor', [(0, 1), (1, 0)])  24.6 us
    unnamed x1, blocking collectives  19.5 us
    all_to_all x1, waiting for transfers between devices, body(): lax.all_to_all(state_own, 'dp', split_axis=0, concat_axis=1, tiled=True)  16.5 us
    ppermute x10, waiting for transfers between devices, swap(): return lax.ppermute(array, 'section', [(0, 1), (1, 0)])  11.3 us
    all_to_all x1, waiting for transfers between devices, body(): lax.all_to_all(tok_full, 'dp', split_axis=1, concat_axis=0, tiled=True)  11.2 us
    all_gather x1, blocking collectives, body(): tok_full = lax.all_gather(tok_half, 'tensor', axis=1, tiled=True)  9.97 us
  transfers between devices with their start and end apart: 19, of which 15 were waited for; matrix products, arithmetic and copies ran while one was open for 6% of the time, Pallas kernels for 0%

commit v1 on v0

--- a/solution.py
+++ b/solution.py
@@ -71,7 +71,14 @@
         pre = lax.psum_scatter(part, "dp", scatter_dimension=0, tiled=True)
         inverse_rms = lax.rsqrt(sums / width + EPS)
         hidden = jax.nn.gelu(pre.astype(F32) * inverse_rms[:, None], approximate=True).astype(BF16)
-        hidden_all = lax.all_gather(hidden, "dp", axis=0, tiled=True)
+        ring = [hidden]
+        for hop in range(7):
+            ring.append(lax.ppermute(ring[-1], "dp", [(dev, (dev + 1) % 8) for dev in range(8)]))
+        hidden_all = jnp.roll(
+            jnp.concatenate(ring[::-1], axis=0),
+            (lax.axis_index("dp") + 1) * ring[0].shape[0],
+            axis=0,
+        )
         hiddens.append(hidden_all)
         out = jnp.dot(hidden_all, down_parts[layer], preferred_element_type=F32)
         mid = all_rows // layers

time: 414 us -> 460 us (1.11)
  waiting for transfers between devices: 288 us -> 322 us
  other arithmetic: 14.5 us -> 22.2 us
  local copies, waits for them, and re-layouts: 22.6 us -> 27.8 us
    ppermute x0 -> x14, waiting for transfers between devices: none -> 144 us  [body(): lax.ppermute(ring[-1], 'dp', [(dev, (dev + 1) % 8) for dev in range(8)])]
    all_gather x2 -> x0, waiting for transfers between devices: 103 us -> none  [body(): hidden_all = lax.all_gather(hidden, 'dp', axis=0, tiled=True)]
    unnamed x30 -> x64, local copies, waits for them, and re-layouts: 8.5 us -> 16.7 us
  transfers between devices with their start and end apart: 19 -> 31, of which waited for: 15 -> 26; matrix products, arithmetic and copies ran while one was open for 6% -> 7% of each run, Pallas kernels for 0% -> 0%
where the time goes in v1:
time: 460 us; the launch traced here: 459 us
  waiting for transfers between devices  322 us (70%)
  blocking collectives  31.9 us (7%)
  local copies, waits for them, and re-layouts  27.8 us (6%)
  other arithmetic  22.2 us (5%)
  starting transfers between devices  21.8 us (5%)
  matrix products  17.9 us (4%)
  between operations  15.2 us (3%)
    ppermute x14, waiting for transfers between devices, body(): lax.ppermute(ring[-1], 'dp', [(dev, (dev + 1) % 8) for dev in range(8)])  144 us
    reduce_scatter x2, waiting for transfers between devices, body(): pre = lax.psum_scatter(part, 'dp', scatter_dimension=0, tiled=True)  116 us
    ppermute x2, waiting for transfers between devices, body(): got = lax.ppermute(sent, 'tensor', [(0, 1), (1, 0)])  23.5 us
    unnamed x1, blocking collectives  17.6 us
    unnamed x64, local copies, waits for them, and re-layouts  16.7 us
    all_to_all x1, waiting for transfers between devices, body(): lax.all_to_all(state_own, 'dp', split_axis=0, concat_axis=1, tiled=True)  13.4 us
    all_to_all x1, waiting for transfers between devices, body(): lax.all_to_all(tok_full, 'dp', split_axis=1, concat_axis=0, tiled=True)  12.1 us
    all_gather x1, blocking collectives, body(): tok_full = lax.all_gather(tok_half, 'tensor', axis=1, tiled=True)  9.97 us
  transfers between devices with their start and end apart: 31, of which 26 were waited for; matrix products, arithmetic and copies ran while one was open for 7% of the time, Pallas kernels for 0%

profile of v1, /device:TPU:0, one launch (start us, length us, event | category | flops | bytes accessed | tf_op | source)
XLA Modules:
  0.0 458.7 jit_solution(12929232081435340537)
XLA Ops:
  8.2 10.0 %all_gather.6 = bf16[64,4096]{1,0:T(8,128)(2,1)S(1)} all-gather(bf16[64,2048]{1,0:T(8,128)(2,1)S(1)} %constant_dynamic-slice_fusion.2), channel_id=1, replica_groups=mesh['section'=2,'dp'=8,'tensor'=2] {'tensor'}, dimensions={1}, use_global_device_ids=true | all-gather | bytes 786432 | tf_op jit(solution)/shard_map/all_gather | solution.py:36
  19.1 6.0 %all-to-all-start = ((bf16[64,8,512]{2,0,1:T(8,128)(2,1)}), bf16[64,8,512]{2,0,1:T(8,128)(2,1)S(1)}, u32[]{:S(2)}, u32[]{:S(2)}) async-start(bf16[64,8,512]{2,0,1:T(8,128)(2,1)} %bitcast.43), calls=%async_computation | async-start | bytes 1048576 | tf_op jit(solution)/shard_map/all_to_all | solution.py:41
  26.6 12.1 %all-to-all-done = bf16[64,8,512]{2,0,1:T(8,128)(2,1)S(1)} async-done(((bf16[64,8,512]{2,0,1:T(8,128)(2,1)}), bf16[64,8,512]{2,0,1:T(8,128)(2,1)S(1)}, u32[]{:S(2)}, u32[]{:S(2)}) %all-to-all-start) | async-done | bytes 524320 | tf_op jit(solution)/shard_map/all_to_all | solution.py:41
  38.8 4.3 all_gather.7
  52.7 68.6 %reduce-scatter.3.cloned.1.call-done = bf16[128,1280]{1,0:T(8,128)(2,1)} async-done(((bf16[1024,1280]{1,0:T(8,128)(2,1)}), bf16[128,1280]{1,0:T(8,128)(2,1)}) %reduce-scatter.3.cloned.1.call-update) | async-done | bytes 327696 | tf_op jit(solution)/shard_map/reduce_scatter | solution.py:71
  123.5 10.0 %collective-permute-done.4 = bf16[128,1280]{1,0:T(8,128)(2,1)S(1)} collective-permute-done((bf16[128,1280]{1,0:T(8,128)(2,1)S(1)}, bf16[128,1280]{1,0:T(8,128)(2,1)S(1)}, u32[]{:S(2)}, u32[]{:S(2)}) %collective-permute-start.4) | collective-permute-done | bytes 327712 | tf_op jit(solution)/shard_map/ppermute | solution.py:76
  133.4 9.9 %collective-permute-done.5 = bf16[128,1280]{1,0:T(8,128)(2,1)S(1)} collective-permute-done((bf16[128,1280]{1,0:T(8,128)(2,1)S(1)}, bf16[128,1280]{1,0:T(8,128)(2,1)S(1)}, u32[]{:S(2)}, u32[]{:S(2)}) %collective-permute-start.5) | collective-permute-done | bytes 327712 | tf_op jit(solution)/shard_map/ppermute | solution.py:76
  143.4 9.8 %collective-permute-done.6 = bf16[128,1280]{1,0:T(8,128)(2,1)S(1)} collective-permute-done((bf16[128,1280]{1,0:T(8,128)(2,1)S(1)}, bf16[128,1280]{1,0:T(8,128)(2,1)S(1)}, u32[]{:S(2)}, u32[]{:S(2)}) %collective-permute-start.6) | collective-permute-done | bytes 327712 | tf_op jit(solution)/shard_map/ppermute | solution.py:76
  153.9 9.8 %collective-permute-done.7 = bf16[128,1280]{1,0:T(8,128)(2,1)S(1)} collective-permute-done((bf16[128,1280]{1,0:T(8,128)(2,1)S(1)}, bf16[128,1280]{1,0:T(8,128)(2,1)S(1)}, u32[]{:S(2)}, u32[]{:S(2)}) %collective-permute-start.7) | collective-permute-done | bytes 327712 | tf_op jit(solution)/shard_map/ppermute | solution.py:76
  164.4 10.4 %collective-permute-done.8 = bf16[128,1280]{1,0:T(8,128)(2,1)S(1)} collective-permute-done((bf16[128,1280]{1,0:T(8,128)(2,1)S(1)}, bf16[128,1280]{1,0:T(8,128)(2,1)S(1)}, u32[]{:S(2)}, u32[]{:S(2)}) %collective-permute-start.8) | collective-permute-done | bytes 327712 | tf_op jit(solution)/shard_map/ppermute | solution.py:76
  175.6 12.1 %collective-permute-done.9 = bf16[128,1280]{1,0:T(8,128)(2,1)} collective-permute-done((bf16[128,1280]{1,0:T(8,128)(2,1)S(1)}, bf16[128,1280]{1,0:T(8,128)(2,1)}, u32[]{:S(2)}, u32[]{:S(2)}) %collective-permute-start.9) | collective-permute-done | bytes 327712 | tf_op jit(solution)/shard_map/ppermute | solution.py:76
  188.8 8.9 %collective-permute-done.10 = bf16[128,1280]{1,0:T(8,128)(2,1)} collective-permute-done((bf16[128,1280]{1,0:T(8,128)(2,1)}, bf16[128,1280]{1,0:T(8,128)(2,1)}, u32[]{:S(2)}, u32[]{:S(2)}) %collective-permute-start.10) | collective-permute-done | bytes 327712 | tf_op jit(solution)/shard_map/ppermute | solution.py:76
  212.1 12.5 %collective-permute-done.13 = bf16[512,512]{1,0:T(8,128)(2,1)S(1)} collective-permute-done((bf16[512,512]{1,0:T(8,128)(2,1)S(1)}, bf16[512,512]{1,0:T(8,128)(2,1)S(1)}, u32[]{:S(2)}, u32[]{:S(2)}) %collective-permute-start.13) | collective-permute-done | bytes 524320 | tf_op jit(solution)/shard_map/ppermute | solution.py:90
  227.6 4.4 convolution_convert_fusion
  235.3 17.6 %all-reduce = f32[1024]{0:T(1024)S(1)} all-reduce(f32[1024]{0:T(1024)S(1)} %multiply_reduce_fusion), channel_id=4, replica_groups=mesh['section'=2,'dp'=8,'tensor'=2] {'dp'}, use_global_device_ids=true, to_apply=%region_4.6.clone | all-reduce | flops 1024 | bytes 8192
  252.9 47.8 %reduce-scatter.5.cloned.1.call-done = bf16[128,1280]{1,0:T(8,128)(2,1)} async-done(((bf16[1024,1280]{1,0:T(8,128)(2,1)}), bf16[128,1280]{1,0:T(8,128)(2,1)}) %reduce-scatter.5.cloned.1.call-update) | async-done | bytes 327696 | tf_op jit(solution)/shard_map/reduce_scatter | solution.py:71
  302.9 10.0 %collective-permute-done.15 = bf16[128,1280]{1,0:T(8,128)(2,1)S(1)} collective-permute-done((bf16[128,1280]{1,0:T(8,128)(2,1)S(1)}, bf16[128,1280]{1,0:T(8,128)(2,1)S(1)}, u32[]{:S(2)}, u32[]{:S(2)}) %collective-permute-start.15) | collective-permute-done | bytes 327712 | tf_op jit(solution)/shard_map/ppermute | solution.py:76
  312.8 9.9 %collective-permute-done.16 = bf16[128,1280]{1,0:T(8,128)(2,1)S(1)} collective-permute-done((bf16[128,1280]{1,0:T(8,128)(2,1)S(1)}, bf16[128,1280]{1,0:T(8,128)(2,1)S(1)}, u32[]{:S(2)}, u32[]{:S(2)}) %collective-permute-start.16) | collective-permute-done | bytes 327712 | tf_op jit(solution)/shard_map/ppermute | solution.py:76
  322.7 9.8 %collective-permute-done.17 = bf16[128,1280]{1,0:T(8,128)(2,1)S(1)} collective-permute-done((bf16[128,1280]{1,0:T(8,128)(2,1)S(1)}, bf16[128,1280]{1,0:T(8,128)(2,1)S(1)}, u32[]{:S(2)}, u32[]{:S(2)}) %collective-permute-start.17) | collective-permute-done | bytes 327712 | tf_op jit(solution)/shard_map/ppermute | solution.py:76
  332.5 10.1 %collective-permute-done.18 = bf16[128,1280]{1,0:T(8,128)(2,1)S(1)} collective-permute-done((bf16[128,1280]{1,0:T(8,128)(2,1)S(1)}, bf16[128,1280]{1,0:T(8,128)(2,1)S(1)}, u32[]{:S(2)}, u32[]{:S(2)}) %collective-permute-start.18) | collective-permute-done | bytes 327712 | tf_op jit(solution)/shard_map/ppermute | solution.py:76
  342.6 11.2 %collective-permute-done.19 = bf16[128,1280]{1,0:T(8,128)(2,1)S(1)} collective-permute-done((bf16[128,1280]{1,0:T(8,128)(2,1)S(1)}, bf16[128,1280]{1,0:T(8,128)(2,1)S(1)}, u32[]{:S(2)}, u32[]{:S(2)}) %collective-permute-start.19) | collective-permute-done | bytes 327712 | tf_op jit(solution)/shard_map/ppermute | solution.py:76
  353.8 12.4 %collective-permute-done.20 = bf16[128,1280]{1,0:T(8,128)(2,1)S(1)} collective-permute-done((bf16[128,1280]{1,0:T(8,128)(2,1)S(1)}, bf16[128,1280]{1,0:T(8,128)(2,1)S(1)}, u32[]{:S(2)}, u32[]{:S(2)}) %collective-permute-start.20) | collective-permute-done | bytes 327712 | tf_op jit(solution)/shard_map/ppermute | solution.py:76
  366.1 9.8 %collective-permute-done.21 = bf16[128,1280]{1,0:T(8,128)(2,1)S(1)} collective-permute-done((bf16[128,1280]{1,0:T(8,128)(2,1)S(1)}, bf16[128,1280]{1,0:T(8,128)(2,1)S(1)}, u32[]{:S(2)}, u32[]{:S(2)}) %collective-permute-start.21) | collective-permute-done | bytes 327712 | tf_op jit(solution)/shard_map/ppermute | solution.py:76
  376.4 4.9 %broadcast_select_fusion.2 = (bf16[1024,1280]{1,0:T(8,128)(2,1)}, bf16[1024,1280]{1,0:T(8,128)(2,1)S(1)}) fusion(pred[]{:T(512)S(6)} %eq.3, s32[]{:T(128)S(6)} %select_n.182, bf16[1024,1280]{1,0:T(8,128)(2,1)S(1)} %constant_dynamic-update-slice_fusion.8, bf16[1024,1280]{1,0:T(8,128)(2,1)S(1)} %constant_dynamic-update-slice_fusion), kind=kLoop, calls=%fused_computation.16 | loop fusion | flops 11796480 | bytes 10485765 | tf_op jit(solution)/shard_map/jit(_where)/select_n | solution.py:103
  381.3 3.8 fusion.13
  389.5 4.3 all-to-all-start.2
  398.2 11.0 %collective-permute-done.23 = bf16[512,512]{1,0:T(8,128)(2,1)S(1)} collective-permute-done((bf16[512,512]{1,0:T(8,128)(2,1)S(1)}, bf16[512,512]{1,0:T(8,128)(2,1)S(1)}, u32[]{:S(2)}, u32[]{:S(2)}) %collective-permute-start.23) | collective-permute-done | bytes 524320 | tf_op jit(solution)/shard_map/ppermute | solution.py:90
  415.0 4.9 %all-to-all-done.2 = bf16[128,8,512]{0,2,1:T(8,128)(2,1)} async-done(((bf16[128,8,512]{0,2,1:T(8,128)(2,1)}), bf16[128,8,512]{0,2,1:T(8,128)(2,1)}, u32[]{:S(2)}, u32[]{:S(2)}) %all-to-all-start.2) | async-done | bytes 1048608 | tf_op jit(solution)/shard_map/all_to_all | solution.py:33
  419.9 4.3 all-to-all-start.1
  426.5 5.6 %broadcast_select_fusion.1 = (bf16[1024,1280]{1,0:T(8,128)(2,1)S(1)}, bf16[1024,1280]{1,0:T(8,128)(2,1)S(1)}) fusion(bf16[1024,1280]{1,0:T(8,128)(2,1)} %collective-permute-done.25, pred[]{:T(512)S(6)} %eq.3, bf16[1024,1280]{1,0:T(8,128)(2,1)} %copy-done.2, s32[]{:T(128)S(6)} %select_n.182, bf16[1024,1280]{1,0:T(8,128)(2,1)S(1)} %constant_dynamic-update-slice_fusion), kind=kLoop, calls=%fused_computation.15 | loop fusion | flops 9175040 | bytes 13107205 | tf_op jit(solution)/shard_map/jit(_where)/select_n | solution.py:31
  432.1 4.3 fusion.7
  436.4 13.4 %all-to-all-done.1 = bf16[8,128,512]{1,2,0:T(8,128)(2,1)} async-done(((bf16[8,128,512]{1,2,0:T(8,128)(2,1)}), bf16[8,128,512]{1,2,0:T(8,128)(2,1)}, u32[]{:S(2)}, u32[]{:S(2)}) %all-to-all-start.1) | async-done | bytes 1048608 | tf_op jit(solution)/shard_map/all_to_all | solution.py:100
  (138 shorter events, 60.0 us)
Async XLA Ops:
  19.1 19.7 %all-to-all-start = ((bf16[64,8,512]{2,0,1:T(8,128)(2,1)}), bf16[64,8,512]{2,0,1:T(8,128)(2,1)S(1)}, u32[]{:S(2)}, u32[]{:S(2)}) async-start(bf16[64,8,512]{2,0,1:T(8,128)(2,1)} %bitcast.43), calls=%async_computation | async-start | bytes 1048576 | tf_op jit(solution)/shard_map/all_to_all | solution.py:41
  25.1 96.2 %reduce-scatter.3.cloned.1.call-start = ((), (), s32[]{:S(2)}) async-start(), calls=%async_computation.5 | async-start | bytes 2949120 | tf_op jit(solution)/shard_map/reduce_scatter | solution.py:71
  26.5 18.4 %collective-permute-start.2 = (bf16[512,1280]{1,0:T(8,128)(2,1)S(1)}, bf16[512,1280]{1,0:T(8,128)(2,1)}, u32[]{:S(2)}, u32[]{:S(2)}) collective-permute-start(bf16[512,1280]{1,0:T(8,128)(2,1)S(1)} %dynamic-slice_bitcast_fusion.1), channel_id=1, source_target_pairs={{0,16},{16,0},{1,17},{17,1},{2,18},{18,2},{3,19},{19,3},{4,20},{20... | collective-permute-start | bytes 3932168 | tf_op jit(solution)/shard_map/ppermute | solution.py:28
  38.7 5.6 %collective-permute-start = (bf16[512,512]{1,0:T(8,128)(2,1)S(1)}, bf16[512,512]{1,0:T(8,128)(2,1)S(1)}, u32[]{:S(2)}, u32[]{:S(2)}) collective-permute-start(bf16[512,512]{1,0:T(8,128)(2,1)S(1)} %bitcast.47), channel_id=1, source_target_pairs={{0,16},{16,0},{1,17},{17,1},{2,18},{18,2},{3,19},{19,3},{4,20},{20... | collective-permute-start | bytes 1572872 | tf_op jit(solution)/shard_map/ppermute | solution.py:28
  43.1 1.2 collective-permute-start.1
  50.0 137.7 %copy-start.14 = (bf16[1,2560,512]{2,1,0:T(8,128)(2,1)S(1)}, bf16[1,2560,512]{2,1,0:T(8,128)(2,1)}, u32[]{:S(2)}) copy-start(bf16[1,2560,512]{2,1,0:T(8,128)(2,1)} %param.10) | copy-start | bytes 7864324
  50.0 250.6 %reduce-scatter.5.cloned.1.call-start = ((), (), s32[]{:S(2)}) async-start(), calls=%async_computation.6 | async-start | bytes 2949120 | tf_op jit(solution)/shard_map/reduce_scatter | solution.py:71
  50.3 2.4 collective-permute-start.3
  122.6 10.9 %collective-permute-start.4 = (bf16[128,1280]{1,0:T(8,128)(2,1)S(1)}, bf16[128,1280]{1,0:T(8,128)(2,1)S(1)}, u32[]{:S(2)}, u32[]{:S(2)}) collective-permute-start(bf16[128,1280]{1,0:T(8,128)(2,1)S(1)} %fusion.32), channel_id=1, source_target_pairs={{0,2},{2,4},{4,6},{6,8},{8,10},{10,12},{12,14},{14,0},{1,3},{3,5},... | collective-permute-start | bytes 983048 | tf_op jit(solution)/shard_map/ppermute | solution.py:76
  133.4 9.9 %collective-permute-start.5 = (bf16[128,1280]{1,0:T(8,128)(2,1)S(1)}, bf16[128,1280]{1,0:T(8,128)(2,1)S(1)}, u32[]{:S(2)}, u32[]{:S(2)}) collective-permute-start(bf16[128,1280]{1,0:T(8,128)(2,1)S(1)} %collective-permute-done.4), channel_id=1, source_target_pairs={{0,2},{2,4},{4,6},{6,8},{8,10},{10,12},{12,14},{14,0},{1,3},{3,5},... | collective-permute-start | bytes 983048 | tf_op jit(solution)/shard_map/ppermute | solution.py:76
  143.4 9.8 %collective-permute-start.6 = (bf16[128,1280]{1,0:T(8,128)(2,1)S(1)}, bf16[128,1280]{1,0:T(8,128)(2,1)S(1)}, u32[]{:S(2)}, u32[]{:S(2)}) collective-permute-start(bf16[128,1280]{1,0:T(8,128)(2,1)S(1)} %collective-permute-done.5), channel_id=1, source_target_pairs={{0,2},{2,4},{4,6},{6,8},{8,10},{10,12},{12,14},{14,0},{1,3},{3,5},... | collective-permute-start | bytes 983048 | tf_op jit(solution)/shard_map/ppermute | solution.py:76
  153.9 9.8 %collective-permute-start.7 = (bf16[128,1280]{1,0:T(8,128)(2,1)S(1)}, bf16[128,1280]{1,0:T(8,128)(2,1)S(1)}, u32[]{:S(2)}, u32[]{:S(2)}) collective-permute-start(bf16[128,1280]{1,0:T(8,128)(2,1)S(1)} %collective-permute-done.6), channel_id=1, source_target_pairs={{0,2},{2,4},{4,6},{6,8},{8,10},{10,12},{12,14},{14,0},{1,3},{3,5},... | collective-permute-start | bytes 983048 | tf_op jit(solution)/shard_map/ppermute | solution.py:76
  164.4 10.4 %collective-permute-start.8 = (bf16[128,1280]{1,0:T(8,128)(2,1)S(1)}, bf16[128,1280]{1,0:T(8,128)(2,1)S(1)}, u32[]{:S(2)}, u32[]{:S(2)}) collective-permute-start(bf16[128,1280]{1,0:T(8,128)(2,1)S(1)} %collective-permute-done.7), channel_id=1, source_target_pairs={{0,2},{2,4},{4,6},{6,8},{8,10},{10,12},{12,14},{14,0},{1,3},{3,5},... | collective-permute-start | bytes 983048 | tf_op jit(solution)/shard_map/ppermute | solution.py:76
  175.6 12.1 %collective-permute-start.9 = (bf16[128,1280]{1,0:T(8,128)(2,1)S(1)}, bf16[128,1280]{1,0:T(8,128)(2,1)}, u32[]{:S(2)}, u32[]{:S(2)}) collective-permute-start(bf16[128,1280]{1,0:T(8,128)(2,1)S(1)} %collective-permute-done.8), channel_id=1, source_target_pairs={{0,2},{2,4},{4,6},{6,8},{8,10},{10,12},{12,14},{14,0},{1,3},{3,5},... | collective-permute-start | bytes 983048 | tf_op jit(solution)/shard_map/ppermute | solution.py:76
  187.7 10.1 %collective-permute-start.10 = (bf16[128,1280]{1,0:T(8,128)(2,1)}, bf16[128,1280]{1,0:T(8,128)(2,1)}, u32[]{:S(2)}, u32[]{:S(2)}) collective-permute-start(bf16[128,1280]{1,0:T(8,128)(2,1)} %collective-permute-done.9), channel_id=1, source_target_pairs={{0,2},{2,4},{4,6},{6,8},{8,10},{10,12},{12,14},{14,0},{1,3},{3,5},... | collective-permute-start | bytes 983048 | tf_op jit(solution)/shard_map/ppermute | solution.py:76
  188.8 14.3 %collective-permute-start.11 = (bf16[1280,512]{1,0:T(8,128)(2,1)}, bf16[1280,512]{1,0:T(8,128)(2,1)}, u32[]{:S(2)}, u32[]{:S(2)}) collective-permute-start(bf16[1280,512]{1,0:T(8,128)(2,1)} %dynamic-slice_bitcast_fusion), channel_id=1, source_target_pairs={{0,16},{16,0},{1,17},{17,1},{2,18},{18,2},{3,19},{19,3},{4,20},{20... | collective-permute-start | bytes 3932168 | tf_op jit(solution)/shard_map/ppermute | solution.py:28
  206.9 2.1 collective-permute-start.12
  210.5 14.0 %collective-permute-start.13 = (bf16[512,512]{1,0:T(8,128)(2,1)S(1)}, bf16[512,512]{1,0:T(8,128)(2,1)S(1)}, u32[]{:S(2)}, u32[]{:S(2)}) collective-permute-start(bf16[512,512]{1,0:T(8,128)(2,1)S(1)} %add_convert_fusion.3), channel_id=1, source_target_pairs={{0,1},{1,0},{2,3},{3,2},{4,5},{5,4},{6,7},{7,6},{8,9},{9,8},{10,11... | collective-permute-start | bytes 1572872 | tf_op jit(solution)/shard_map/ppermute | solution.py:90
  224.8 2.0 collective-permute-start.14
  302.0 10.8 %collective-permute-start.15 = (bf16[128,1280]{1,0:T(8,128)(2,1)S(1)}, bf16[128,1280]{1,0:T(8,128)(2,1)S(1)}, u32[]{:S(2)}, u32[]{:S(2)}) collective-permute-start(bf16[128,1280]{1,0:T(8,128)(2,1)S(1)} %fusion.40), channel_id=1, source_target_pairs={{0,2},{2,4},{4,6},{6,8},{8,10},{10,12},{12,14},{14,0},{1,3},{3,5},... | collective-permute-start | bytes 983048 | tf_op jit(solution)/shard_map/ppermute | solution.py:76
  312.8 9.9 %collective-permute-start.16 = (bf16[128,1280]{1,0:T(8,128)(2,1)S(1)}, bf16[128,1280]{1,0:T(8,128)(2,1)S(1)}, u32[]{:S(2)}, u32[]{:S(2)}) collective-permute-start(bf16[128,1280]{1,0:T(8,128)(2,1)S(1)} %collective-permute-done.15), channel_id=1, source_target_pairs={{0,2},{2,4},{4,6},{6,8},{8,10},{10,12},{12,14},{14,0},{1,3},{3,5},... | collective-permute-start | bytes 983048 | tf_op jit(solution)/shard_map/ppermute | solution.py:76
  322.7 9.8 %collective-permute-start.17 = (bf16[128,1280]{1,0:T(8,128)(2,1)S(1)}, bf16[128,1280]{1,0:T(8,128)(2,1)S(1)}, u32[]{:S(2)}, u32[]{:S(2)}) collective-permute-start(bf16[128,1280]{1,0:T(8,128)(2,1)S(1)} %collective-permute-done.16), channel_id=1, source_target_pairs={{0,2},{2,4},{4,6},{6,8},{8,10},{10,12},{12,14},{14,0},{1,3},{3,5},... | collective-permute-start | bytes 983048 | tf_op jit(solution)/shard_map/ppermute | solution.py:76
  332.5 10.1 %collective-permute-start.18 = (bf16[128,1280]{1,0:T(8,128)(2,1)S(1)}, bf16[128,1280]{1,0:T(8,128)(2,1)S(1)}, u32[]{:S(2)}, u32[]{:S(2)}) collective-permute-start(bf16[128,1280]{1,0:T(8,128)(2,1)S(1)} %collective-permute-done.17), channel_id=1, source_target_pairs={{0,2},{2,4},{4,6},{6,8},{8,10},{10,12},{12,14},{14,0},{1,3},{3,5},... | collective-permute-start | bytes 983048 | tf_op jit(solution)/shard_map/ppermute | solution.py:76
  342.5 11.2 %collective-permute-start.19 = (bf16[128,1280]{1,0:T(8,128)(2,1)S(1)}, bf16[128,1280]{1,0:T(8,128)(2,1)S(1)}, u32[]{:S(2)}, u32[]{:S(2)}) collective-permute-start(bf16[128,1280]{1,0:T(8,128)(2,1)S(1)} %collective-permute-done.18), channel_id=1, source_target_pairs={{0,2},{2,4},{4,6},{6,8},{8,10},{10,12},{12,14},{14,0},{1,3},{3,5},... | collective-permute-start | bytes 983048 | tf_op jit(solution)/shard_map/ppermute | solution.py:76
  353.8 12.4 %collective-permute-start.20 = (bf16[128,1280]{1,0:T(8,128)(2,1)S(1)}, bf16[128,1280]{1,0:T(8,128)(2,1)S(1)}, u32[]{:S(2)}, u32[]{:S(2)}) collective-permute-start(bf16[128,1280]{1,0:T(8,128)(2,1)S(1)} %collective-permute-done.19), channel_id=1, source_target_pairs={{0,2},{2,4},{4,6},{6,8},{8,10},{10,12},{12,14},{14,0},{1,3},{3,5},... | collective-permute-start | bytes 983048 | tf_op jit(solution)/shard_map/ppermute | solution.py:76
  366.1 9.8 %collective-permute-start.21 = (bf16[128,1280]{1,0:T(8,128)(2,1)S(1)}, bf16[128,1280]{1,0:T(8,128)(2,1)S(1)}, u32[]{:S(2)}, u32[]{:S(2)}) collective-permute-start(bf16[128,1280]{1,0:T(8,128)(2,1)S(1)} %collective-permute-done.20), channel_id=1, source_target_pairs={{0,2},{2,4},{4,6},{6,8},{8,10},{10,12},{12,14},{14,0},{1,3},{3,5},... | collective-permute-start | bytes 983048 | tf_op jit(solution)/shard_map/ppermute | solution.py:76
  386.7 7.1 %collective-permute-start.22 = (bf16[512,512]{1,0:T(8,128)(2,1)}, bf16[512,512]{1,0:T(8,128)(2,1)}, u32[]{:S(2)}, u32[]{:S(2)}) collective-permute-start(bf16[512,512]{1,0:T(8,128)(2,1)} %dynamic-slice_convert_fusion), channel_id=1, source_target_pairs={{0,16},{16,0},{1,17},{17,1},{2,18},{18,2},{3,19},{19,3},{4,20},{20... | collective-permute-start | bytes 1572872 | tf_op jit(solution)/shard_map/ppermute | solution.py:28
  386.7 39.8 %collective-permute-start.25 = (bf16[1024,1280]{1,0:T(8,128)(2,1)}, bf16[1024,1280]{1,0:T(8,128)(2,1)}, u32[]{:S(2)}, u32[]{:S(2)}) collective-permute-start(bf16[1024,1280]{1,0:T(8,128)(2,1)} %get-tuple-element.3), channel_id=1, source_target_pairs={{0,16},{16,0},{1,17},{17,1},{2,18},{18,2},{3,19},{19,3},{4,20},{20... | collective-permute-start | bytes 7864328 | tf_op jit(solution)/shard_map/ppermute | solution.py:28
  389.5 30.5 %all-to-all-start.2 = ((bf16[128,8,512]{0,2,1:T(8,128)(2,1)}), bf16[128,8,512]{0,2,1:T(8,128)(2,1)}, u32[]{:S(2)}, u32[]{:S(2)}) async-start(bf16[128,8,512]{0,2,1:T(8,128)(2,1)} %bitcast.45), calls=%async_computation.4 | async-start | bytes 2097152 | tf_op jit(solution)/shard_map/all_to_all | solution.py:33
  395.3 13.9 %collective-permute-start.23 = (bf16[512,512]{1,0:T(8,128)(2,1)S(1)}, bf16[512,512]{1,0:T(8,128)(2,1)S(1)}, u32[]{:S(2)}, u32[]{:S(2)}) collective-permute-start(bf16[512,512]{1,0:T(8,128)(2,1)S(1)} %add_convert_fusion.1), channel_id=1, source_target_pairs={{0,1},{1,0},{2,3},{3,2},{4,5},{5,4},{6,7},{7,6},{8,9},{9,8},{10,11... | collective-permute-start | bytes 1572872 | tf_op jit(solution)/shard_map/ppermute | solution.py:90
  409.4 2.0 collective-permute-start.24
  419.9 29.8 %all-to-all-start.1 = ((bf16[8,128,512]{1,2,0:T(8,128)(2,1)}), bf16[8,128,512]{1,2,0:T(8,128)(2,1)}, u32[]{:S(2)}, u32[]{:S(2)}) async-start(bf16[8,128,512]{1,2,0:T(8,128)(2,1)} %copy.16), calls=%async_computation.3 | async-start | bytes 2097152 | tf_op jit(solution)/shard_map/all_to_all | solution.py:100
  (23 other events, 286.0 us)
Sparse Core Ops, SparseCore 0:
  50.2 71.0 reduce-scatter.2
  232.2 68.4 reduce-scatter.4
